TPU v7x, 128 devices: a whole 4x4x4 slice. The times are simulated.
128 devices in a mesh: band: 32 (over y, x_hi, z), grid: 4 (over x_lo, core).
Axes of the slice: x: 4 (x_hi: 2, x_lo: 2; x = x_hi * 2 + x_lo), y: 4, z: 4, core: 2. Of those that a mesh axis runs over, the one named last changes fastest.
Arguments:
- orbitals: float32 [96, 64, 4096], P('band', 'grid'), may hold values from -6 to 6
- pair_mask: int32 [96, 96], replicated, may hold values from 0 to 1, as said below
Outputs:
- exchange_term: float32 [96, 64, 4096], P('band', 'grid')
Inputs may be any that keep to these rules, and one draw needn't show every extreme that they name: pair_mask is symmetric; entries outside the candidate pairs of every block (and their transposes) are 0; each block has at most 12 candidate pairs with mask 1, and some block has exactly 12.
All inputs are finite; a program needn't handle non-finite values.
Results may differ from a plain program's by a relative error of at most 0.00027.
Values sent between devices are 32-bit elements; how exact they have to be, the bound alone decides.
A program may use at most 64 MiB of HBM per device.

v0:
```python
import math
import jax
import jax.numpy as jnp
import numpy as np
from jax import lax
from jax.sharding import PartitionSpec as P

NG = 64
ORB_DEV = 3
REACH = 2
NCAND = 24
CAP = 12
MIXING = 0.25
BOX_LENGTH = 16.0
EXACT_PRECISION = lax.Precision.HIGHEST
turn_pairs = 4


def shifted(block, axis, distance):
    devices = range(lax.axis_size(axis))
    route = [((i - distance) % len(devices), i) for i in devices]
    return lax.ppermute(block, axis, route)


def pair_table():
    entries = []
    for distance in range(REACH + 1):
        for leading_orbital in range(ORB_DEV):
            for second_orb in range(ORB_DEV):
                if distance > 0 or leading_orbital <= second_orb:
                    entries.append((leading_orbital, distance, second_orb))
    return np.array(entries, dtype=np.int32)


def dft_tables(length):
    positions = jnp.arange(length, dtype=jnp.int32)
    product_mod = positions[:, None] * positions[None, :] % length
    angles = product_mod.astype(jnp.float32) * (2.0 * math.pi / length)
    return (jnp.cos(angles), jnp.sin(angles))


def rotate_parts(values_in):
    half_width = values_in.shape[-1] // 2
    return jnp.concatenate([values_in[..., half_width:], -values_in[..., :half_width]], axis=-1)


def transform_axis(values_in, tables, formula, sweep_direction):
    cosine_table, sine_table = tables
    direct_part = jnp.einsum(formula, cosine_table, values_in, precision=EXACT_PRECISION)
    crossed_part = jnp.einsum(formula, sine_table, values_in, precision=EXACT_PRECISION)
    return direct_part + sweep_direction * rotate_parts(crossed_part)


def signed_frequency(positions):
    return jnp.where(positions < NG // 2, positions, positions - NG)


def coulomb_values(squared):
    safe_values = jnp.maximum(squared, 1).astype(jnp.float32)
    return jnp.where(squared > 0, BOX_LENGTH * BOX_LENGTH / math.pi / safe_values, 0.0)


def solve_poisson(density, tables, kernel_pair, z_tables):
    count_pairs = density.shape[0]
    planes = density.shape[1]
    cubes = density.reshape(count_pairs, planes, NG, NG)
    joined = jnp.concatenate([cubes[0::2], cubes[1::2]], axis=-1)
    spectrum = jnp.einsum("pxyz,zk->pxyk", joined, z_tables[0], precision=EXACT_PRECISION)
    spectrum = transform_axis(spectrum, tables, "ky,pxyc->pxkc", 1.0)
    columns = lax.all_to_all(spectrum, "grid", split_axis=2, concat_axis=1, tiled=True)
    columns = transform_axis(columns, tables, "kx,pxyc->pkyc", 1.0)
    columns = columns * kernel_pair[None]
    columns = transform_axis(columns, tables, "kx,pxyc->pkyc", -1.0)
    returned = lax.all_to_all(columns, "grid", split_axis=1, concat_axis=2, tiled=True)
    returned = transform_axis(returned, tables, "ky,pxyc->pxkc", -1.0)
    fields = jnp.einsum("pxyc,ck->pxyk", returned, z_tables[2], precision=EXACT_PRECISION)
    potential = jnp.stack([fields[..., :NG], fields[..., NG:]], axis=1)
    return potential.reshape(count_pairs, planes, NG * NG)


def local(orbitals, pair_mask):
    orb_count, planes, cells = orbitals.shape
    groups = lax.axis_size("band")
    band_index = lax.axis_index("band")
    grid_index = lax.axis_index("grid")
    visits = [orbitals]
    for distance in range(1, REACH + 1):
        visits.append(shifted(orbitals, "band", -distance))
    flat_count = (REACH + 1) * orb_count
    flat_visiting = jnp.stack(visits).reshape(flat_count, planes, cells)
    pair_list = pair_table()
    first_ids = jnp.asarray(pair_list[:, 0])
    offsets = jnp.asarray(pair_list[:, 1])
    second_ids = jnp.asarray(pair_list[:, 2])
    row_ids = band_index * ORB_DEV + first_ids
    col_ids = (band_index + offsets) % groups * ORB_DEV + second_ids
    live_flags = pair_mask[row_ids, col_ids]
    sort_keys = (1 - live_flags) * NCAND + jnp.arange(NCAND, dtype=jnp.int32)
    live_order = jnp.argsort(sort_keys)[:CAP]
    first_ids = first_ids[live_order]
    offsets = offsets[live_order]
    second_ids = second_ids[live_order]
    live_flags = live_flags[live_order]
    padding = -first_ids.shape[0] % turn_pairs

    def padded(values_in):
        return jnp.concatenate([values_in, jnp.zeros((padding,), jnp.int32)])

    first_ids = padded(first_ids)
    offsets = padded(offsets)
    second_ids = padded(second_ids)
    live_flags = padded(live_flags)
    slot_ids = offsets * ORB_DEV + second_ids
    weights = live_flags.astype(jnp.float32)
    self_flags = 1.0 - ((offsets == 0) & (first_ids == second_ids)).astype(jnp.float32)
    turns = first_ids.shape[0] // turn_pairs
    tables = dft_tables(NG)
    cosine_table, sine_table = tables
    forward_complex = jnp.block([[cosine_table, -sine_table], [sine_table, cosine_table]])
    forward_real = jnp.concatenate([cosine_table, -sine_table], axis=1)
    inverse_complex = jnp.block([[cosine_table, sine_table], [-sine_table, cosine_table]])
    inverse_real = jnp.concatenate([cosine_table, -sine_table], axis=0)
    z_tables = (forward_complex, forward_real, inverse_complex, inverse_real)
    waves_first = signed_frequency(jnp.arange(NG, dtype=jnp.int32))[:, None, None]
    waves_second = signed_frequency(grid_index * planes + jnp.arange(planes, dtype=jnp.int32))[
        None, :, None
    ]
    waves_third = signed_frequency(jnp.arange(NG, dtype=jnp.int32))[None, None, :]
    kernel = coulomb_values(
        waves_first * waves_first + waves_second * waves_second + waves_third * waves_third
    ) / float(NG**3)
    kernel_pair = jnp.concatenate([kernel, kernel], axis=-1)

    def one_turn(totals, turn_input):
        owned_total, visit_total = totals
        first_turn, slot_turn, weight_turn, self_turn = turn_input
        leading_orbital = orbitals[first_turn]
        second_orb = flat_visiting[slot_turn]
        potential = solve_poisson(leading_orbital * second_orb, tables, kernel_pair, z_tables)
        weighted_density = potential * weight_turn[:, None, None]
        owner_hot = (first_turn[:, None] == jnp.arange(orb_count, dtype=jnp.int32)[None, :]).astype(
            jnp.float32
        )
        visit_onehot_mask = (
            slot_turn[:, None] == jnp.arange(flat_count, dtype=jnp.int32)[None, :]
        ).astype(jnp.float32) * self_turn[:, None]
        owned_total = owned_total + jnp.einsum(
            "pa,pxc->axc", owner_hot, weighted_density * second_orb, precision=EXACT_PRECISION
        )
        visit_total = visit_total + jnp.einsum(
            "sq,swt->qwt",
            visit_onehot_mask,
            weighted_density * leading_orbital,
            precision=EXACT_PRECISION,
        )
        return ((owned_total, visit_total), None)

    start_totals = (
        jnp.zeros((orb_count, planes, cells), jnp.float32),
        jnp.zeros((flat_count, planes, cells), jnp.float32),
    )
    turn_inputs = (
        first_ids.reshape(turns, turn_pairs),
        slot_ids.reshape(turns, turn_pairs),
        weights.reshape(turns, turn_pairs),
        self_flags.reshape(turns, turn_pairs),
    )
    (owned_total, visit_total), discarded_value = lax.scan(one_turn, start_totals, turn_inputs)
    visit_total = visit_total.reshape(REACH + 1, orb_count, planes, cells)
    owned = owned_total + visit_total[0]
    for distance in range(1, REACH + 1):
        owned = owned + shifted(visit_total[distance], "band", distance)
    return -MIXING * owned


def solution(mesh):
    return jax.shard_map(
        local,
        mesh=mesh,
        in_specs=(P("band", "grid", None), P()),
        out_specs=P("band", "grid", None),
        check_vma=False,
    )
```

profile of v0, /device:TPU:0, one launch (start us, length us, event | category | flops | bytes accessed | tf_op | source)
XLA Modules:
  0.0 318.8 jit_solution(15074602083450062132)
XLA Ops:
  0.0 8.9 %collective-permute-start.1 = (f32[3,16,4096]{2,1,0:T(8,128)}, f32[3,16,4096]{2,1,0:T(8,128)S(1)}, u32[]{:S(2)}, u32[]{:S(2)}) collective-permute-start(f32[3,16,4096]{2,1,0:T(8,128)} %param.7), channel_id=1, source_target_pairs={{8,0},{12,4},{16,8},{20,12},{24,16},{28,20},{32,24},{36,28},{40,32... | collective-permute-start | bytes 2359304 | tf_op jit(solution)/shard_map/ppermute | solution.py:22
  19.6 7.6 %collective-permute-done.1 = f32[3,16,4096]{2,1,0:T(8,128)S(1)} collective-permute-done((f32[3,16,4096]{2,1,0:T(8,128)}, f32[3,16,4096]{2,1,0:T(8,128)S(1)}, u32[]{:S(2)}, u32[]{:S(2)}) %collective-permute-start.1) | collective-permute-done | bytes 786464 | tf_op jit(solution)/shard_map/ppermute | solution.py:22
  27.2 16.1 %collective-permute-done = f32[3,16,4096]{2,1,0:T(8,128)S(1)} collective-permute-done((f32[3,16,4096]{2,1,0:T(8,128)}, f32[3,16,4096]{2,1,0:T(8,128)S(1)}, u32[]{:S(2)}, u32[]{:S(2)}) %collective-permute-start) | collective-permute-done | bytes 786464 | tf_op jit(solution)/shard_map/ppermute | solution.py:22
  44.9 226.3 %while.14 = (s32[]{:T(128)}, f32[3,16,4096]{2,0,1:T(4,128)}, f32[9,16,4096]{2,0,1:T(8,128)}, s32[3,4]{1,0:T(4,128)S(1)}, f32[3,16,4096]{2,1,0:T(8,128)S(1)}, /*i...) while((s32[]{:T(128)}, f32[3,16,4096]{2,0,1:T(4,128)}, ...), condition=%wide.region_2.3_spmd.clone.clone, body=%wide.region_1.2_spmd.clone.clone.sunk | while | flops 2460682240 | bytes 111813288 | solution.py:168
  45.6 2.3 gather_fusion.1
  48.0 2.2 mul.862
  56.6 16.9 %all_to_all.48 = f32[2,16,64,128]{3,1,0,2:T(8,128)S(1)} all-to-all(f32[2,16,64,128]{3,1,0,2:T(8,128)S(1)} %copy.52), channel_id=1, replica_groups=mesh['band'=32,'grid'=4] {'grid'}, dimensions={2} | all-to-all | bytes 2097152 | tf_op jit(solution)/shard_map/while/body/eval_jaxpr/all_to_all | solution.py:70
  81.9 3.5 %all-to-all-start.1 = ((f32[2,64,16,128]{3,2,0,1:T(8,128)}), f32[2,64,16,128]{3,2,0,1:T(8,128)S(1)}, u32[]{:S(2)}, u32[]{:S(2)}) async-start(f32[2,64,16,128]{3,2,0,1:T(8,128)} %copy.54), calls=%async_computation.1 | async-start | bytes 2097152 | tf_op jit(solution)/shard_map/while/body/eval_jaxpr/all_to_all | solution.py:74
  85.5 14.4 %all-to-all-done.1 = f32[2,64,16,128]{3,2,0,1:T(8,128)S(1)} async-done(((f32[2,64,16,128]{3,2,0,1:T(8,128)}), f32[2,64,16,128]{3,2,0,1:T(8,128)S(1)}, u32[]{:S(2)}, u32[]{:S(2)}) %all-to-all-start.1) | async-done | bytes 1048608 | tf_op jit(solution)/shard_map/while/body/eval_jaxpr/all_to_all | solution.py:74
  106.2 2.1 reshape.255
  109.5 2.5 convolution_add_fusion.4
  112.0 6.4 %convolution_add_fusion.5 = f32[9,16,4096]{2,0,1:T(8,128)S(1)} fusion(f32[9,16,4096]{2,0,1:T(8,128)S(1)} %copy-done.1, pred[]{:T(512)S(6)} %compare.9, f32[4,16,4096]{2,1,0:T(8,128)S(1)} %get-tuple-element.342, f32[4]{0:T(128)S(1)} %get-tuple-element.343, s32[4]{0:T(128)S(1)} %get-tuple-element.344), kind=kOutput, calls=%fused_computation.9.clone.1 | convolution fusion | flops 29491272 | bytes 5767201 | tf_op jit(solution)/shard_map/while/body/eval_jaxpr/sq,swt->qwt/dot_general | solution.py:150
  121.0 2.3 gather_fusion.1
  123.4 2.2 mul.862
  132.0 16.9 %all_to_all.48 = f32[2,16,64,128]{3,1,0,2:T(8,128)S(1)} all-to-all(f32[2,16,64,128]{3,1,0,2:T(8,128)S(1)} %copy.52), channel_id=1, replica_groups=mesh['band'=32,'grid'=4] {'grid'}, dimensions={2} | all-to-all | bytes 2097152 | tf_op jit(solution)/shard_map/while/body/eval_jaxpr/all_to_all | solution.py:70
  157.4 3.5 %all-to-all-start.1 = ((f32[2,64,16,128]{3,2,0,1:T(8,128)}), f32[2,64,16,128]{3,2,0,1:T(8,128)S(1)}, u32[]{:S(2)}, u32[]{:S(2)}) async-start(f32[2,64,16,128]{3,2,0,1:T(8,128)} %copy.54), calls=%async_computation.1 | async-start | bytes 2097152 | tf_op jit(solution)/shard_map/while/body/eval_jaxpr/all_to_all | solution.py:74
  160.9 14.4 %all-to-all-done.1 = f32[2,64,16,128]{3,2,0,1:T(8,128)S(1)} async-done(((f32[2,64,16,128]{3,2,0,1:T(8,128)}), f32[2,64,16,128]{3,2,0,1:T(8,128)S(1)}, u32[]{:S(2)}, u32[]{:S(2)}) %all-to-all-start.1) | async-done | bytes 1048608 | tf_op jit(solution)/shard_map/while/body/eval_jaxpr/all_to_all | solution.py:74
  181.6 2.1 reshape.255
  185.0 2.5 convolution_add_fusion.4
  187.4 6.4 %convolution_add_fusion.5 = f32[9,16,4096]{2,0,1:T(8,128)S(1)} fusion(f32[9,16,4096]{2,0,1:T(8,128)S(1)} %copy-done.1, pred[]{:T(512)S(6)} %compare.9, f32[4,16,4096]{2,1,0:T(8,128)S(1)} %get-tuple-element.342, f32[4]{0:T(128)S(1)} %get-tuple-element.343, s32[4]{0:T(128)S(1)} %get-tuple-element.344), kind=kOutput, calls=%fused_computation.9.clone.1 | convolution fusion | flops 29491272 | bytes 5767201 | tf_op jit(solution)/shard_map/while/body/eval_jaxpr/sq,swt->qwt/dot_general | solution.py:150
  196.5 2.3 gather_fusion.1
  198.9 2.2 mul.862
  207.5 16.9 %all_to_all.48 = f32[2,16,64,128]{3,1,0,2:T(8,128)S(1)} all-to-all(f32[2,16,64,128]{3,1,0,2:T(8,128)S(1)} %copy.52), channel_id=1, replica_groups=mesh['band'=32,'grid'=4] {'grid'}, dimensions={2} | all-to-all | bytes 2097152 | tf_op jit(solution)/shard_map/while/body/eval_jaxpr/all_to_all | solution.py:70
  232.8 3.5 %all-to-all-start.1 = ((f32[2,64,16,128]{3,2,0,1:T(8,128)}), f32[2,64,16,128]{3,2,0,1:T(8,128)S(1)}, u32[]{:S(2)}, u32[]{:S(2)}) async-start(f32[2,64,16,128]{3,2,0,1:T(8,128)} %copy.54), calls=%async_computation.1 | async-start | bytes 2097152 | tf_op jit(solution)/shard_map/while/body/eval_jaxpr/all_to_all | solution.py:74
  236.4 14.4 %all-to-all-done.1 = f32[2,64,16,128]{3,2,0,1:T(8,128)S(1)} async-done(((f32[2,64,16,128]{3,2,0,1:T(8,128)}), f32[2,64,16,128]{3,2,0,1:T(8,128)S(1)}, u32[]{:S(2)}, u32[]{:S(2)}) %all-to-all-start.1) | async-done | bytes 1048608 | tf_op jit(solution)/shard_map/while/body/eval_jaxpr/all_to_all | solution.py:74
  257.0 2.1 reshape.255
  260.4 2.5 convolution_add_fusion.4
  262.9 6.4 %convolution_add_fusion.5 = f32[9,16,4096]{2,0,1:T(8,128)S(1)} fusion(f32[9,16,4096]{2,0,1:T(8,128)S(1)} %copy-done.1, pred[]{:T(512)S(6)} %compare.9, f32[4,16,4096]{2,1,0:T(8,128)S(1)} %get-tuple-element.342, f32[4]{0:T(128)S(1)} %get-tuple-element.343, s32[4]{0:T(128)S(1)} %get-tuple-element.344), kind=kOutput, calls=%fused_computation.9.clone.1 | convolution fusion | flops 29491272 | bytes 5767201 | tf_op jit(solution)/shard_map/while/body/eval_jaxpr/sq,swt->qwt/dot_general | solution.py:150
  271.2 3.6 %copy.30 = f32[9,16,4096]{2,1,0:T(8,128)S(1)} copy(f32[9,16,4096]{2,0,1:T(8,128)} %get-tuple-element.394) | data formatting | bytes 4718592 | tf_op jit(solution)/shard_map/while | solution.py:168
  275.0 2.2 collective-permute-start.2
  277.2 23.2 %collective-permute-done.3 = f32[3,16,4096]{2,1,0:T(8,128)S(1)} collective-permute-done((f32[3,16,4096]{2,1,0:T(8,128)S(1)}, f32[3,16,4096]{2,1,0:T(8,128)S(1)}, u32[]{:S(2)}, u32[]{:S(2)}) %collective-permute-start.3) | collective-permute-done | bytes 786464 | tf_op jit(solution)/shard_map/ppermute | solution.py:22
  300.4 16.9 %collective-permute-done.2 = f32[3,16,4096]{2,1,0:T(8,128)S(1)} collective-permute-done((f32[3,16,4096]{2,1,0:T(8,128)S(1)}, f32[3,16,4096]{2,1,0:T(8,128)S(1)}, u32[]{:S(2)}, u32[]{:S(2)}) %collective-permute-start.2) | collective-permute-done | bytes 786464 | tf_op jit(solution)/shard_map/ppermute | solution.py:22
  (168 shorter events, 88.7 us)
Async XLA Ops:
  0.0 10.3 %copy-start = (s32[96,96]{1,0:T(8,128)S(1)}, s32[96,96]{1,0:T(8,128)}, u32[]{:S(2)}) copy-start(s32[96,96]{1,0:T(8,128)} %param.8) | copy-start | bytes 110596
  0.0 43.3 %copy-start.3 = (f32[3,16,4096]{2,1,0:T(8,128)S(1)}, f32[3,16,4096]{2,1,0:T(8,128)}, u32[]{:S(2)}) copy-start(f32[3,16,4096]{2,1,0:T(8,128)} %param.7) | copy-start | bytes 2359300
  0.0 27.1 %collective-permute-start.1 = (f32[3,16,4096]{2,1,0:T(8,128)}, f32[3,16,4096]{2,1,0:T(8,128)S(1)}, u32[]{:S(2)}, u32[]{:S(2)}) collective-permute-start(f32[3,16,4096]{2,1,0:T(8,128)} %param.7), channel_id=1, source_target_pairs={{8,0},{12,4},{16,8},{20,12},{24,16},{28,20},{32,24},{36,28},{40,32... | collective-permute-start | bytes 2359304 | tf_op jit(solution)/shard_map/ppermute | solution.py:22
  8.9 34.4 %collective-permute-start = (f32[3,16,4096]{2,1,0:T(8,128)}, f32[3,16,4096]{2,1,0:T(8,128)S(1)}, u32[]{:S(2)}, u32[]{:S(2)}) collective-permute-start(f32[3,16,4096]{2,1,0:T(8,128)} %param.7), channel_id=1, source_target_pairs={{4,0},{8,4},{12,8},{16,12},{20,16},{24,20},{28,24},{32,28},{36,32}... | collective-permute-start | bytes 2359304 | tf_op jit(solution)/shard_map/ppermute | solution.py:22
  74.8 1.0 copy-start.8
  81.9 17.9 %all-to-all-start.1 = ((f32[2,64,16,128]{3,2,0,1:T(8,128)}), f32[2,64,16,128]{3,2,0,1:T(8,128)S(1)}, u32[]{:S(2)}, u32[]{:S(2)}) async-start(f32[2,64,16,128]{3,2,0,1:T(8,128)} %copy.54), calls=%async_computation.1 | async-start | bytes 2097152 | tf_op jit(solution)/shard_map/while/body/eval_jaxpr/all_to_all | solution.py:74
  108.3 1.2 copy-start.5
  108.3 3.7 %copy-start.1 = (f32[9,16,4096]{2,0,1:T(8,128)S(1)}, f32[9,16,4096]{2,0,1:T(8,128)}, u32[]{:S(2)}) copy-start(f32[9,16,4096]{2,0,1:T(8,128)} %get-tuple-element.361) | copy-start | bytes 7077892 | tf_op jit(solution)/shard_map/while
  112.0 6.4 %copy-start.6 = (f32[3,16,4096]{2,0,1:T(4,128)}, f32[3,16,4096]{2,0,1:T(4,128)S(1)}, u32[]{:S(2)}) copy-start(f32[3,16,4096]{2,0,1:T(4,128)S(1)} %convolution_add_fusion.4) | copy-start | bytes 2359300 | tf_op jit(solution)/shard_map/while
  112.0 8.4 %copy-start.4 = (f32[3,16,4096]{2,1,0:T(8,128)S(1)}, f32[3,16,4096]{2,1,0:T(8,128)}, u32[]{:S(2)}) copy-start(f32[3,16,4096]{2,1,0:T(8,128)} %get-tuple-element.406) | copy-start | bytes 2359300 | tf_op jit(solution)/shard_map/while
  118.4 1.9 copy-start.2
  150.2 1.0 copy-start.8
  157.4 17.9 %all-to-all-start.1 = ((f32[2,64,16,128]{3,2,0,1:T(8,128)}), f32[2,64,16,128]{3,2,0,1:T(8,128)S(1)}, u32[]{:S(2)}, u32[]{:S(2)}) async-start(f32[2,64,16,128]{3,2,0,1:T(8,128)} %copy.54), calls=%async_computation.1 | async-start | bytes 2097152 | tf_op jit(solution)/shard_map/while/body/eval_jaxpr/all_to_all | solution.py:74
  183.7 1.2 copy-start.5
  183.7 3.7 %copy-start.1 = (f32[9,16,4096]{2,0,1:T(8,128)S(1)}, f32[9,16,4096]{2,0,1:T(8,128)}, u32[]{:S(2)}) copy-start(f32[9,16,4096]{2,0,1:T(8,128)} %get-tuple-element.361) | copy-start | bytes 7077892 | tf_op jit(solution)/shard_map/while
  187.4 6.4 %copy-start.6 = (f32[3,16,4096]{2,0,1:T(4,128)}, f32[3,16,4096]{2,0,1:T(4,128)S(1)}, u32[]{:S(2)}) copy-start(f32[3,16,4096]{2,0,1:T(4,128)S(1)} %convolution_add_fusion.4) | copy-start | bytes 2359300 | tf_op jit(solution)/shard_map/while
  187.4 8.4 %copy-start.4 = (f32[3,16,4096]{2,1,0:T(8,128)S(1)}, f32[3,16,4096]{2,1,0:T(8,128)}, u32[]{:S(2)}) copy-start(f32[3,16,4096]{2,1,0:T(8,128)} %get-tuple-element.406) | copy-start | bytes 2359300 | tf_op jit(solution)/shard_map/while
  193.9 1.9 copy-start.2
  225.6 1.0 copy-start.8
  232.8 17.9 %all-to-all-start.1 = ((f32[2,64,16,128]{3,2,0,1:T(8,128)}), f32[2,64,16,128]{3,2,0,1:T(8,128)S(1)}, u32[]{:S(2)}, u32[]{:S(2)}) async-start(f32[2,64,16,128]{3,2,0,1:T(8,128)} %copy.54), calls=%async_computation.1 | async-start | bytes 2097152 | tf_op jit(solution)/shard_map/while/body/eval_jaxpr/all_to_all | solution.py:74
  259.2 1.2 copy-start.5
  259.2 3.7 %copy-start.1 = (f32[9,16,4096]{2,0,1:T(8,128)S(1)}, f32[9,16,4096]{2,0,1:T(8,128)}, u32[]{:S(2)}) copy-start(f32[9,16,4096]{2,0,1:T(8,128)} %get-tuple-element.361) | copy-start | bytes 7077892 | tf_op jit(solution)/shard_map/while
  262.9 6.4 %copy-start.6 = (f32[3,16,4096]{2,0,1:T(4,128)}, f32[3,16,4096]{2,0,1:T(4,128)S(1)}, u32[]{:S(2)}) copy-start(f32[3,16,4096]{2,0,1:T(4,128)S(1)} %convolution_add_fusion.4) | copy-start | bytes 2359300 | tf_op jit(solution)/shard_map/while
  262.9 8.4 %copy-start.4 = (f32[3,16,4096]{2,1,0:T(8,128)S(1)}, f32[3,16,4096]{2,1,0:T(8,128)}, u32[]{:S(2)}) copy-start(f32[3,16,4096]{2,1,0:T(8,128)} %get-tuple-element.406) | copy-start | bytes 2359300 | tf_op jit(solution)/shard_map/while
  269.3 1.9 copy-start.2
  274.8 42.6 %copy-start.7 = (f32[3,16,4096]{2,0,1:T(4,128)S(1)}, f32[3,16,4096]{2,0,1:T(4,128)}, u32[]{:S(2)}) copy-start(f32[3,16,4096]{2,0,1:T(4,128)} %get-tuple-element.393) | copy-start | bytes 2359300
  274.9 25.5 %collective-permute-start.3 = (f32[3,16,4096]{2,1,0:T(8,128)S(1)}, f32[3,16,4096]{2,1,0:T(8,128)S(1)}, u32[]{:S(2)}, u32[]{:S(2)}) collective-permute-start(f32[3,16,4096]{2,1,0:T(8,128)S(1)} %get-tuple-element.227), channel_id=1, source_target_pairs={{120,0},{124,4},{0,8},{4,12},{8,16},{12,20},{16,24},{20,28},{24,32... | collective-permute-start | bytes 2359304 | tf_op jit(solution)/shard_map/ppermute | solution.py:22
  275.0 42.3 %collective-permute-start.2 = (f32[3,16,4096]{2,1,0:T(8,128)S(1)}, f32[3,16,4096]{2,1,0:T(8,128)S(1)}, u32[]{:S(2)}, u32[]{:S(2)}) collective-permute-start(f32[3,16,4096]{2,1,0:T(8,128)S(1)} %get-tuple-element.226), channel_id=1, source_target_pairs={{124,0},{0,4},{4,8},{8,12},{12,16},{16,20},{20,24},{24,28},{28,32}... | collective-permute-start | bytes 2359304 | tf_op jit(solution)/shard_map/ppermute | solution.py:22
where the time goes:
time: 320 us; the launch traced here: 319 us
  waiting for transfers between devices  107 us (33%)
  matrix products  64 us (20%)
  local copies, waits for them, and re-layouts  59.6 us (19%)
  blocking collectives  50.6 us (16%)
  starting transfers between devices  22.5 us (7%)
  other arithmetic  14.3 us (4%)
    ppermute x4, waiting for transfers between devices, shifted(): return lax.ppermute(block, axis, route)  63.8 us
    all_to_all x3, blocking collectives, solve_poisson(): lax.all_to_all(spectrum, 'grid', split_axis=2, concat_axis=1, tiled=True)  50.6 us
    all_to_all x3, waiting for transfers between devices, solve_poisson(): lax.all_to_all(columns, 'grid', split_axis=1, concat_axis=2, tiled=True)  43.1 us
    dot_general x3, matrix products, one_turn(): jnp.einsum('sq,swt->qwt', visit_onehot_mask, weighted_density * leading_o...  19.2 us
    dot_general x12, matrix products, transform_axis(): jnp.einsum(formula, cosine_table, values_in, precision=EXACT_PRECISION)  17.1 us
    dot_general x12, matrix products, transform_axis(): jnp.einsum(formula, sine_table, values_in, precision=EXACT_PRECISION)  14.2 us
    ppermute x4, starting transfers between devices, shifted(): return lax.ppermute(block, axis, route)  11.9 us
    all_to_all x3, starting transfers between devices, solve_poisson(): lax.all_to_all(columns, 'grid', split_axis=1, concat_axis=2, tiled=True)  10.5 us
  transfers between devices with their start and end apart: 7, of which 7 were waited for; matrix products, arithmetic and copies ran while one was open for 3% of the time, Pallas kernels for 0%

commit v1 on v0

--- a/solution.py
+++ b/solution.py
@@ -67,7 +67,10 @@
     joined = jnp.concatenate([cubes[0::2], cubes[1::2]], axis=-1)
     spectrum = jnp.einsum("pxyz,zk->pxyk", joined, z_tables[0], precision=EXACT_PRECISION)
     spectrum = transform_axis(spectrum, tables, "ky,pxyc->pxkc", 1.0)
-    columns = lax.all_to_all(spectrum, "grid", split_axis=2, concat_axis=1, tiled=True)
+    columns = jnp.concatenate(
+        lax.all_to_all(jnp.stack(jnp.split(spectrum, lax.axis_size("grid"), axis=2)), "grid", 0, 0),
+        axis=1,
+    )
     columns = transform_axis(columns, tables, "kx,pxyc->pkyc", 1.0)
     columns = columns * kernel_pair[None]
     columns = transform_axis(columns, tables, "kx,pxyc->pkyc", -1.0)

time: 320 us -> 320 us (level)
    add x6 -> x3, local copies, waits for them, and re-layouts: 6.53 us -> 4.73 us  [transform_axis(): return direct_part + sweep_direction * rotate_parts(crossed_part)]
where the time goes in v1:
time: 320 us; the launch traced here: 319 us
  waiting for transfers between devices  107 us (33%)
  matrix products  65.4 us (20%)
  local copies, waits for them, and re-layouts  57.9 us (18%)
  blocking collectives  50.6 us (16%)
  starting transfers between devices  22.5 us (7%)
  other arithmetic  14.5 us (5%)
    ppermute x4, waiting for transfers between devices, shifted(): return lax.ppermute(block, axis, route)  63.8 us
    all_to_all x3, blocking collectives, solve_poisson(): lax.all_to_all(jnp.stack(jnp.split(spectrum, lax.axis_size('grid'), axis=...  50.6 us
    all_to_all x3, waiting for transfers between devices, solve_poisson(): lax.all_to_all(columns, 'grid', split_axis=1, concat_axis=2, tiled=True)  43.1 us
    dot_general x3, matrix products, one_turn(): jnp.einsum('sq,swt->qwt', visit_onehot_mask, weighted_density * leading_o...  19.2 us
    dot_general x12, matrix products, transform_axis(): jnp.einsum(formula, cosine_table, values_in, precision=EXACT_PRECISION)  17.8 us
    dot_general x12, matrix products, transform_axis(): jnp.einsum(formula, sine_table, values_in, precision=EXACT_PRECISION)  14.9 us
    ppermute x4, starting transfers between devices, shifted(): return lax.ppermute(block, axis, route)  11.9 us
    all_to_all x3, starting transfers between devices, solve_poisson(): lax.all_to_all(columns, 'grid', split_axis=1, concat_axis=2, tiled=True)  10.5 us
  transfers between devices with their start and end apart: 7, of which 7 were waited for; matrix products, arithmetic and copies ran while one was open for 3% of the time, Pallas kernels for 0%

profile of v1, /device:TPU:0, one launch (start us, length us, event | category | flops | bytes accessed | tf_op | source)
XLA Modules:
  0.0 318.8 jit_solution(9582572326664614585)
XLA Ops:
  0.0 8.9 %collective-permute-start.1 = (f32[3,16,4096]{2,1,0:T(8,128)}, f32[3,16,4096]{2,1,0:T(8,128)S(1)}, u32[]{:S(2)}, u32[]{:S(2)}) collective-permute-start(f32[3,16,4096]{2,1,0:T(8,128)} %param.7), channel_id=1, source_target_pairs={{8,0},{12,4},{16,8},{20,12},{24,16},{28,20},{32,24},{36,28},{40,32... | collective-permute-start | bytes 2359304 | tf_op jit(solution)/shard_map/ppermute | solution.py:22
  19.6 7.6 %collective-permute-done.1 = f32[3,16,4096]{2,1,0:T(8,128)S(1)} collective-permute-done((f32[3,16,4096]{2,1,0:T(8,128)}, f32[3,16,4096]{2,1,0:T(8,128)S(1)}, u32[]{:S(2)}, u32[]{:S(2)}) %collective-permute-start.1) | collective-permute-done | bytes 786464 | tf_op jit(solution)/shard_map/ppermute | solution.py:22
  27.2 16.1 %collective-permute-done = f32[3,16,4096]{2,1,0:T(8,128)S(1)} collective-permute-done((f32[3,16,4096]{2,1,0:T(8,128)}, f32[3,16,4096]{2,1,0:T(8,128)S(1)}, u32[]{:S(2)}, u32[]{:S(2)}) %collective-permute-start) | collective-permute-done | bytes 786464 | tf_op jit(solution)/shard_map/ppermute | solution.py:22
  44.9 226.3 %while.14 = (s32[]{:T(128)}, f32[3,16,4096]{2,0,1:T(4,128)}, f32[9,16,4096]{2,0,1:T(8,128)}, s32[3,4]{1,0:T(4,128)S(1)}, f32[3,16,4096]{2,1,0:T(8,128)S(1)}, /*i...) while((s32[]{:T(128)}, f32[3,16,4096]{2,0,1:T(4,128)}, ...), condition=%wide.region_2.3_spmd.clone.clone, body=%wide.region_1.2_spmd.clone.clone.sunk | while | flops 2461468672 | bytes 113910440 | solution.py:171
  45.6 2.3 gather_fusion.1
  48.0 2.2 mul.862
  56.2 16.9 %all_to_all.32 = f32[4,2,16,16,128]{4,3,2,1,0:T(8,128)S(1)} all-to-all(f32[4,2,16,16,128]{4,3,2,1,0:T(8,128)S(1)} %pad_maximum_fusion.10), channel_id=1, replica_groups=mesh['band'=32,'grid'=4] {'grid'}, dimensions={0} | all-to-all | bytes 2097152 | tf_op jit(solution)/shard_map/while/body/eval_jaxpr/all_to_all | solution.py:71
  81.9 3.5 %all-to-all-start.1 = ((f32[2,64,16,128]{3,2,0,1:T(8,128)}), f32[2,64,16,128]{3,2,0,1:T(8,128)S(1)}, u32[]{:S(2)}, u32[]{:S(2)}) async-start(f32[2,64,16,128]{3,2,0,1:T(8,128)} %copy.62), calls=%async_computation.1 | async-start | bytes 2097152 | tf_op jit(solution)/shard_map/while/body/eval_jaxpr/all_to_all | solution.py:77
  85.5 14.4 %all-to-all-done.1 = f32[2,64,16,128]{3,2,0,1:T(8,128)S(1)} async-done(((f32[2,64,16,128]{3,2,0,1:T(8,128)}), f32[2,64,16,128]{3,2,0,1:T(8,128)S(1)}, u32[]{:S(2)}, u32[]{:S(2)}) %all-to-all-start.1) | async-done | bytes 1048608 | tf_op jit(solution)/shard_map/while/body/eval_jaxpr/all_to_all | solution.py:77
  106.2 2.1 reshape.265
  109.5 2.5 convolution_add_fusion.4
  112.0 6.4 %convolution_add_fusion.5 = f32[9,16,4096]{2,0,1:T(8,128)S(1)} fusion(f32[9,16,4096]{2,0,1:T(8,128)S(1)} %copy-done.1, pred[]{:T(512)S(6)} %compare.9, f32[4,16,4096]{2,1,0:T(8,128)S(1)} %get-tuple-element.354, f32[4]{0:T(128)S(1)} %get-tuple-element.355, s32[4]{0:T(128)S(1)} %get-tuple-element.356), kind=kOutput, calls=%fused_computation.9.clone.1 | convolution fusion | flops 29491272 | bytes 5767201 | tf_op jit(solution)/shard_map/while/body/eval_jaxpr/sq,swt->qwt/dot_general | solution.py:153
  121.0 2.3 gather_fusion.1
  123.4 2.2 mul.862
  131.6 16.9 %all_to_all.32 = f32[4,2,16,16,128]{4,3,2,1,0:T(8,128)S(1)} all-to-all(f32[4,2,16,16,128]{4,3,2,1,0:T(8,128)S(1)} %pad_maximum_fusion.10), channel_id=1, replica_groups=mesh['band'=32,'grid'=4] {'grid'}, dimensions={0} | all-to-all | bytes 2097152 | tf_op jit(solution)/shard_map/while/body/eval_jaxpr/all_to_all | solution.py:71
  157.4 3.5 %all-to-all-start.1 = ((f32[2,64,16,128]{3,2,0,1:T(8,128)}), f32[2,64,16,128]{3,2,0,1:T(8,128)S(1)}, u32[]{:S(2)}, u32[]{:S(2)}) async-start(f32[2,64,16,128]{3,2,0,1:T(8,128)} %copy.62), calls=%async_computation.1 | async-start | bytes 2097152 | tf_op jit(solution)/shard_map/while/body/eval_jaxpr/all_to_all | solution.py:77
  160.9 14.4 %all-to-all-done.1 = f32[2,64,16,128]{3,2,0,1:T(8,128)S(1)} async-done(((f32[2,64,16,128]{3,2,0,1:T(8,128)}), f32[2,64,16,128]{3,2,0,1:T(8,128)S(1)}, u32[]{:S(2)}, u32[]{:S(2)}) %all-to-all-start.1) | async-done | bytes 1048608 | tf_op jit(solution)/shard_map/while/body/eval_jaxpr/all_to_all | solution.py:77
  181.6 2.1 reshape.265
  185.0 2.5 convolution_add_fusion.4
  187.4 6.4 %convolution_add_fusion.5 = f32[9,16,4096]{2,0,1:T(8,128)S(1)} fusion(f32[9,16,4096]{2,0,1:T(8,128)S(1)} %copy-done.1, pred[]{:T(512)S(6)} %compare.9, f32[4,16,4096]{2,1,0:T(8,128)S(1)} %get-tuple-element.354, f32[4]{0:T(128)S(1)} %get-tuple-element.355, s32[4]{0:T(128)S(1)} %get-tuple-element.356), kind=kOutput, calls=%fused_computation.9.clone.1 | convolution fusion | flops 29491272 | bytes 5767201 | tf_op jit(solution)/shard_map/while/body/eval_jaxpr/sq,swt->qwt/dot_general | solution.py:153
  196.4 2.3 gather_fusion.1
  198.9 2.2 mul.862
  207.0 16.9 %all_to_all.32 = f32[4,2,16,16,128]{4,3,2,1,0:T(8,128)S(1)} all-to-all(f32[4,2,16,16,128]{4,3,2,1,0:T(8,128)S(1)} %pad_maximum_fusion.10), channel_id=1, replica_groups=mesh['band'=32,'grid'=4] {'grid'}, dimensions={0} | all-to-all | bytes 2097152 | tf_op jit(solution)/shard_map/while/body/eval_jaxpr/all_to_all | solution.py:71
  232.8 3.5 %all-to-all-start.1 = ((f32[2,64,16,128]{3,2,0,1:T(8,128)}), f32[2,64,16,128]{3,2,0,1:T(8,128)S(1)}, u32[]{:S(2)}, u32[]{:S(2)}) async-start(f32[2,64,16,128]{3,2,0,1:T(8,128)} %copy.62), calls=%async_computation.1 | async-start | bytes 2097152 | tf_op jit(solution)/shard_map/while/body/eval_jaxpr/all_to_all | solution.py:77
  236.4 14.4 %all-to-all-done.1 = f32[2,64,16,128]{3,2,0,1:T(8,128)S(1)} async-done(((f32[2,64,16,128]{3,2,0,1:T(8,128)}), f32[2,64,16,128]{3,2,0,1:T(8,128)S(1)}, u32[]{:S(2)}, u32[]{:S(2)}) %all-to-all-start.1) | async-done | bytes 1048608 | tf_op jit(solution)/shard_map/while/body/eval_jaxpr/all_to_all | solution.py:77
  257.0 2.1 reshape.265
  260.4 2.5 convolution_add_fusion.4
  262.9 6.4 %convolution_add_fusion.5 = f32[9,16,4096]{2,0,1:T(8,128)S(1)} fusion(f32[9,16,4096]{2,0,1:T(8,128)S(1)} %copy-done.1, pred[]{:T(512)S(6)} %compare.9, f32[4,16,4096]{2,1,0:T(8,128)S(1)} %get-tuple-element.354, f32[4]{0:T(128)S(1)} %get-tuple-element.355, s32[4]{0:T(128)S(1)} %get-tuple-element.356), kind=kOutput, calls=%fused_computation.9.clone.1 | convolution fusion | flops 29491272 | bytes 5767201 | tf_op jit(solution)/shard_map/while/body/eval_jaxpr/sq,swt->qwt/dot_general | solution.py:153
  271.2 3.6 %copy.32 = f32[9,16,4096]{2,1,0:T(8,128)S(1)} copy(f32[9,16,4096]{2,0,1:T(8,128)} %get-tuple-element.406) | data formatting | bytes 4718592 | tf_op jit(solution)/shard_map/while | solution.py:171
  275.0 2.2 collective-permute-start.2
  277.2 23.2 %collective-permute-done.3 = f32[3,16,4096]{2,1,0:T(8,128)S(1)} collective-permute-done((f32[3,16,4096]{2,1,0:T(8,128)S(1)}, f32[3,16,4096]{2,1,0:T(8,128)S(1)}, u32[]{:S(2)}, u32[]{:S(2)}) %collective-permute-start.3) | collective-permute-done | bytes 786464 | tf_op jit(solution)/shard_map/ppermute | solution.py:22
  300.4 16.9 %collective-permute-done.2 = f32[3,16,4096]{2,1,0:T(8,128)S(1)} collective-permute-done((f32[3,16,4096]{2,1,0:T(8,128)S(1)}, f32[3,16,4096]{2,1,0:T(8,128)S(1)}, u32[]{:S(2)}, u32[]{:S(2)}) %collective-permute-start.2) | collective-permute-done | bytes 786464 | tf_op jit(solution)/shard_map/ppermute | solution.py:22
  (171 shorter events, 88.6 us)
Async XLA Ops:
  0.0 10.3 %copy-start = (s32[96,96]{1,0:T(8,128)S(1)}, s32[96,96]{1,0:T(8,128)}, u32[]{:S(2)}) copy-start(s32[96,96]{1,0:T(8,128)} %param.8) | copy-start | bytes 110596
  0.0 43.3 %copy-start.3 = (f32[3,16,4096]{2,1,0:T(8,128)S(1)}, f32[3,16,4096]{2,1,0:T(8,128)}, u32[]{:S(2)}) copy-start(f32[3,16,4096]{2,1,0:T(8,128)} %param.7) | copy-start | bytes 2359300
  0.0 27.1 %collective-permute-start.1 = (f32[3,16,4096]{2,1,0:T(8,128)}, f32[3,16,4096]{2,1,0:T(8,128)S(1)}, u32[]{:S(2)}, u32[]{:S(2)}) collective-permute-start(f32[3,16,4096]{2,1,0:T(8,128)} %param.7), channel_id=1, source_target_pairs={{8,0},{12,4},{16,8},{20,12},{24,16},{28,20},{32,24},{36,28},{40,32... | collective-permute-start | bytes 2359304 | tf_op jit(solution)/shard_map/ppermute | solution.py:22
  8.9 34.4 %collective-permute-start = (f32[3,16,4096]{2,1,0:T(8,128)}, f32[3,16,4096]{2,1,0:T(8,128)S(1)}, u32[]{:S(2)}, u32[]{:S(2)}) collective-permute-start(f32[3,16,4096]{2,1,0:T(8,128)} %param.7), channel_id=1, source_target_pairs={{4,0},{8,4},{12,8},{16,12},{20,16},{24,20},{28,24},{32,28},{36,32}... | collective-permute-start | bytes 2359304 | tf_op jit(solution)/shard_map/ppermute | solution.py:22
  74.5 1.0 copy-start.8
  81.9 17.9 %all-to-all-start.1 = ((f32[2,64,16,128]{3,2,0,1:T(8,128)}), f32[2,64,16,128]{3,2,0,1:T(8,128)S(1)}, u32[]{:S(2)}, u32[]{:S(2)}) async-start(f32[2,64,16,128]{3,2,0,1:T(8,128)} %copy.62), calls=%async_computation.1 | async-start | bytes 2097152 | tf_op jit(solution)/shard_map/while/body/eval_jaxpr/all_to_all | solution.py:77
  108.3 1.2 copy-start.5
  108.3 3.7 %copy-start.1 = (f32[9,16,4096]{2,0,1:T(8,128)S(1)}, f32[9,16,4096]{2,0,1:T(8,128)}, u32[]{:S(2)}) copy-start(f32[9,16,4096]{2,0,1:T(8,128)} %get-tuple-element.373) | copy-start | bytes 7077892 | tf_op jit(solution)/shard_map/while
  112.0 6.4 %copy-start.6 = (f32[3,16,4096]{2,0,1:T(4,128)}, f32[3,16,4096]{2,0,1:T(4,128)S(1)}, u32[]{:S(2)}) copy-start(f32[3,16,4096]{2,0,1:T(4,128)S(1)} %convolution_add_fusion.4) | copy-start | bytes 2359300 | tf_op jit(solution)/shard_map/while
  112.0 8.4 %copy-start.4 = (f32[3,16,4096]{2,1,0:T(8,128)S(1)}, f32[3,16,4096]{2,1,0:T(8,128)}, u32[]{:S(2)}) copy-start(f32[3,16,4096]{2,1,0:T(8,128)} %get-tuple-element.418) | copy-start | bytes 2359300 | tf_op jit(solution)/shard_map/while
  118.4 1.9 copy-start.2
  150.0 1.0 copy-start.8
  157.4 17.9 %all-to-all-start.1 = ((f32[2,64,16,128]{3,2,0,1:T(8,128)}), f32[2,64,16,128]{3,2,0,1:T(8,128)S(1)}, u32[]{:S(2)}, u32[]{:S(2)}) async-start(f32[2,64,16,128]{3,2,0,1:T(8,128)} %copy.62), calls=%async_computation.1 | async-start | bytes 2097152 | tf_op jit(solution)/shard_map/while/body/eval_jaxpr/all_to_all | solution.py:77
  183.7 1.2 copy-start.5
  183.7 3.7 %copy-start.1 = (f32[9,16,4096]{2,0,1:T(8,128)S(1)}, f32[9,16,4096]{2,0,1:T(8,128)}, u32[]{:S(2)}) copy-start(f32[9,16,4096]{2,0,1:T(8,128)} %get-tuple-element.373) | copy-start | bytes 7077892 | tf_op jit(solution)/shard_map/while
  187.4 6.4 %copy-start.6 = (f32[3,16,4096]{2,0,1:T(4,128)}, f32[3,16,4096]{2,0,1:T(4,128)S(1)}, u32[]{:S(2)}) copy-start(f32[3,16,4096]{2,0,1:T(4,128)S(1)} %convolution_add_fusion.4) | copy-start | bytes 2359300 | tf_op jit(solution)/shard_map/while
  187.4 8.4 %copy-start.4 = (f32[3,16,4096]{2,1,0:T(8,128)S(1)}, f32[3,16,4096]{2,1,0:T(8,128)}, u32[]{:S(2)}) copy-start(f32[3,16,4096]{2,1,0:T(8,128)} %get-tuple-element.418) | copy-start | bytes 2359300 | tf_op jit(solution)/shard_map/while
  193.8 1.9 copy-start.2
  225.4 1.0 copy-start.8
  232.8 17.9 %all-to-all-start.1 = ((f32[2,64,16,128]{3,2,0,1:T(8,128)}), f32[2,64,16,128]{3,2,0,1:T(8,128)S(1)}, u32[]{:S(2)}, u32[]{:S(2)}) async-start(f32[2,64,16,128]{3,2,0,1:T(8,128)} %copy.62), calls=%async_computation.1 | async-start | bytes 2097152 | tf_op jit(solution)/shard_map/while/body/eval_jaxpr/all_to_all | solution.py:77
  259.2 1.2 copy-start.5
  259.2 3.7 %copy-start.1 = (f32[9,16,4096]{2,0,1:T(8,128)S(1)}, f32[9,16,4096]{2,0,1:T(8,128)}, u32[]{:S(2)}) copy-start(f32[9,16,4096]{2,0,1:T(8,128)} %get-tuple-element.373) | copy-start | bytes 7077892 | tf_op jit(solution)/shard_map/while
  262.9 6.4 %copy-start.6 = (f32[3,16,4096]{2,0,1:T(4,128)}, f32[3,16,4096]{2,0,1:T(4,128)S(1)}, u32[]{:S(2)}) copy-start(f32[3,16,4096]{2,0,1:T(4,128)S(1)} %convolution_add_fusion.4) | copy-start | bytes 2359300 | tf_op jit(solution)/shard_map/while
  262.9 8.4 %copy-start.4 = (f32[3,16,4096]{2,1,0:T(8,128)S(1)}, f32[3,16,4096]{2,1,0:T(8,128)}, u32[]{:S(2)}) copy-start(f32[3,16,4096]{2,1,0:T(8,128)} %get-tuple-element.418) | copy-start | bytes 2359300 | tf_op jit(solution)/shard_map/while
  269.3 1.9 copy-start.2
  274.8 42.6 %copy-start.7 = (f32[3,16,4096]{2,0,1:T(4,128)S(1)}, f32[3,16,4096]{2,0,1:T(4,128)}, u32[]{:S(2)}) copy-start(f32[3,16,4096]{2,0,1:T(4,128)} %get-tuple-element.405) | copy-start | bytes 2359300
  274.9 25.5 %collective-permute-start.3 = (f32[3,16,4096]{2,1,0:T(8,128)S(1)}, f32[3,16,4096]{2,1,0:T(8,128)S(1)}, u32[]{:S(2)}, u32[]{:S(2)}) collective-permute-start(f32[3,16,4096]{2,1,0:T(8,128)S(1)} %get-tuple-element.231), channel_id=1, source_target_pairs={{120,0},{124,4},{0,8},{4,12},{8,16},{12,20},{16,24},{20,28},{24,32... | collective-permute-start | bytes 2359304 | tf_op jit(solution)/shard_map/ppermute | solution.py:22
  275.0 42.3 %collective-permute-start.2 = (f32[3,16,4096]{2,1,0:T(8,128)S(1)}, f32[3,16,4096]{2,1,0:T(8,128)S(1)}, u32[]{:S(2)}, u32[]{:S(2)}) collective-permute-start(f32[3,16,4096]{2,1,0:T(8,128)S(1)} %get-tuple-element.230), channel_id=1, source_target_pairs={{124,0},{0,4},{4,8},{8,12},{12,16},{16,20},{20,24},{24,28},{28,32}... | collective-permute-start | bytes 2359304 | tf_op jit(solution)/shard_map/ppermute | solution.py:22
